TPU v7x, 32 devices: a whole 2x2x4 slice. The times are simulated.
32 devices in a mesh: dp: 1, ep: 32 (over z, y, x, core).
Axes of the slice: x: 2, y: 2, z: 4, core: 2. Of those that a mesh axis runs over, the one named last changes fastest.
Arguments:
- tokens: bfloat16 [256, 1024], P(('dp', 'ep')), may hold values from -6 to 6
- expert_ids: int32 [256, 8], P(('dp', 'ep')), may hold values from 0 to 31, all different within a row; in each aligned block of 8 rows (0 to 7, 8 to 15, ...) at most 4 rows name the same one
- gate_quant: int32 [256, 8], P(('dp', 'ep')), may hold values from 1 to 1024
- bucket_ids: int32 [256], P(('dp', 'ep')), may hold values from 0 to 15
- bucket_counts: int32 [16], replicated, may hold values from 0 to 512
- gate_weight: bfloat16 [32, 1024, 384], P('ep', 'dp'), may hold values from -0.1875 to 0.1875
- up_weight: bfloat16 [32, 1024, 384], P('ep', 'dp'), may hold values from -0.1875 to 0.1875
- down_weight: bfloat16 [32, 384, 1024], P('ep', 'dp'), may hold values from -0.3125 to 0.3125
- cotangent: bfloat16 [256, 1024], P(('dp', 'ep')), may hold values from -6 to 6
Outputs:
- layer_out: bfloat16 [256, 1024], P(('dp', 'ep'))
- token_grad: bfloat16 [256, 1024], P(('dp', 'ep'))
- gate_grad: float32 [32, 1024, 384], P('ep', 'dp')
- up_grad: float32 [32, 1024, 384], P('ep', 'dp')
- down_grad: float32 [32, 384, 1024], P('ep', 'dp')
Inputs may be any that keep to these rules, and one draw needn't show every extreme that they name: `expert_ids`: each row names 8 different experts. Among the 8 rows of one device no expert is named by more than 4 rows, and in every draw some expert is named by exactly 4 rows of some device.
All inputs are finite; a program needn't handle non-finite values.
Results may differ from a plain program's by a relative error of at most 0.0085.
Values may be sent and summed in bfloat16 or wider, within the bound.
A program may use at most 64 MiB of HBM per device.

v0:
```python
import jax
import jax.numpy as jnp
from jax import lax
from jax.sharding import PartitionSpec as P


def silu_parts(pre_gate):
    sigmoid_val = jax.nn.sigmoid(pre_gate)
    return (pre_gate * sigmoid_val, sigmoid_val * (1.0 + pre_gate * (1.0 - sigmoid_val)))


def contract_rows(left_rows, right_rows):
    return lax.dot_general(
        left_rows, right_rows, (((0,), (0,)), ((), ())), preferred_element_type=jnp.float32
    )


def contract_cols(left_rows, right_rows):
    return lax.dot_general(
        left_rows, right_rows, (((1,), (1,)), ((), ())), preferred_element_type=jnp.float32
    )


def expert_forward(rows_in, gate_full, up_full, down_full):
    pre_gate = jnp.dot(rows_in, gate_full, preferred_element_type=jnp.float32)
    pre_up = jnp.dot(rows_in, up_full, preferred_element_type=jnp.float32)
    activation, derivative = silu_parts(pre_gate)
    hidden = (activation * pre_up).astype(jnp.bfloat16)
    expert_out = jnp.dot(hidden, down_full, preferred_element_type=jnp.float32).astype(jnp.bfloat16)
    return (expert_out, (pre_up, activation, derivative, hidden))


def expert_backward(rows_in, scaled, saved, gate_full, up_full, down_full):
    pre_up, activation, derivative, hidden = saved
    hidden_grad = contract_cols(scaled, down_full)
    gate_pre = (hidden_grad * pre_up * derivative).astype(jnp.bfloat16)
    up_pre = (hidden_grad * activation).astype(jnp.bfloat16)
    slot_grad = (contract_cols(gate_pre, gate_full) + contract_cols(up_pre, up_full)).astype(
        jnp.bfloat16
    )
    return (
        slot_grad,
        contract_rows(rows_in, gate_pre),
        contract_rows(rows_in, up_pre),
        contract_rows(hidden, scaled),
    )


def slot_table(flat_ids, experts, slot_cap):
    total_pairs = flat_ids.shape[0]
    onehot = (flat_ids[:, None] == jnp.arange(experts, dtype=jnp.int32)[None, :]).astype(jnp.int32)
    before = jnp.cumsum(onehot, axis=0) - onehot
    position = jnp.sum(before * onehot, axis=1)
    slot_of = flat_ids * slot_cap + position
    lookup = jnp.full((experts * slot_cap,), total_pairs, jnp.int32)
    lookup = lookup.at[slot_of].set(jnp.arange(total_pairs, dtype=jnp.int32))
    return (lookup, slot_of)


def per_device(
    tokens,
    expert_ids,
    gate_quant,
    bucket_ids,
    bucket_counts,
    gate_weight,
    up_weight,
    down_weight,
    cotangent,
):
    experts = lax.axis_size("ep")
    tok_rows, top_count = expert_ids.shape
    model_width = tokens.shape[1]
    slot_cap = min(tok_rows, 2 * tok_rows * top_count // experts)
    gate_share = gate_quant.astype(jnp.float32) / 1024.0
    bucket_match = (
        bucket_ids[:, None] == jnp.arange(bucket_counts.shape[0], dtype=jnp.int32)[None, :]
    ).astype(jnp.float32)
    count_of = jnp.sum(bucket_match * bucket_counts.astype(jnp.float32)[None, :], axis=1)
    token_scale = 64.0 / (64.0 + count_of)
    flat_ids = expert_ids.reshape(-1)
    total_pairs = flat_ids.shape[0]
    lookup, slot_of = slot_table(flat_ids, experts, slot_cap)
    is_live = lookup < total_pairs
    safe_index = jnp.where(is_live, lookup, 0)
    source_row = safe_index // top_count
    send_rows = jnp.where(is_live[:, None], tokens[source_row], jnp.zeros((), jnp.bfloat16))
    send_rows = send_rows.reshape(experts, slot_cap, model_width)
    scaled_flat = (gate_share * token_scale[:, None]).reshape(-1)
    scale_slot = jnp.where(is_live, scaled_flat[safe_index], jnp.zeros((), jnp.float32))
    send_grads = (scale_slot[:, None] * cotangent[source_row].astype(jnp.float32)).astype(
        jnp.bfloat16
    )
    send_grads = send_grads.reshape(experts, slot_cap, model_width)
    gate_full, up_full, down_full = (
        lax.all_gather(gate_weight, "dp", axis=1, tiled=True),
        lax.all_gather(up_weight, "dp", axis=1, tiled=True),
        lax.all_gather(down_weight, "dp", axis=1, tiled=True),
    )
    gate_full = gate_full[0]
    up_full = up_full[0]
    down_full = down_full[0]
    recv_rows = lax.all_to_all(send_rows, "ep", split_axis=0, concat_axis=0, tiled=True)
    rows_in = recv_rows.reshape(-1, model_width)
    expert_out, saved = expert_forward(rows_in, gate_full, up_full, down_full)
    out_back = lax.all_to_all(
        expert_out.reshape(experts, slot_cap, model_width),
        "ep",
        split_axis=0,
        concat_axis=0,
        tiled=True,
    )
    recv_grads = lax.all_to_all(send_grads, "ep", split_axis=0, concat_axis=0, tiled=True)
    scaled = recv_grads.reshape(-1, model_width)
    slot_grad, grad_gate, grad_up, grad_down = expert_backward(
        rows_in, scaled, saved, gate_full, up_full, down_full
    )
    grad_back = lax.all_to_all(
        slot_grad.reshape(experts, slot_cap, model_width),
        "ep",
        split_axis=0,
        concat_axis=0,
        tiled=True,
    )
    out_pairs = out_back.reshape(experts * slot_cap, model_width)[slot_of].astype(jnp.float32)
    out_pairs = out_pairs.reshape(tok_rows, top_count, model_width)
    layer_out = jnp.sum(gate_share[:, :, None] * out_pairs, axis=1).astype(jnp.bfloat16)
    grad_pairs = grad_back.reshape(experts * slot_cap, model_width)[slot_of].astype(jnp.float32)
    token_grad = jnp.sum(grad_pairs.reshape(tok_rows, top_count, model_width), axis=1).astype(
        jnp.bfloat16
    )
    summed = (
        lax.psum_scatter(
            grad_gate[None].astype(jnp.bfloat16), "dp", scatter_dimension=1, tiled=True
        ).astype(jnp.float32),
        lax.psum_scatter(
            grad_up[None].astype(jnp.bfloat16), "dp", scatter_dimension=1, tiled=True
        ).astype(jnp.float32),
        lax.psum_scatter(
            grad_down[None].astype(jnp.bfloat16), "dp", scatter_dimension=1, tiled=True
        ).astype(jnp.float32),
    )
    return (layer_out, token_grad, summed[0], summed[1], summed[2])


def solution(mesh):
    placed = (
        P(("dp", "ep"), None),
        P(("dp", "ep"), None),
        P(("dp", "ep"), None),
        P(("dp", "ep")),
        P(),
        P("ep", "dp", None),
        P("ep", "dp", None),
        P("ep", "dp", None),
        P(("dp", "ep"), None),
    )
    return jax.shard_map(
        per_device,
        mesh=mesh,
        in_specs=placed,
        out_specs=(
            P(("dp", "ep"), None),
            P(("dp", "ep"), None),
            P("ep", "dp", None),
            P("ep", "dp", None),
            P("ep", "dp", None),
        ),
        check_vma=False,
    )
```

profile of v0, /device:TPU:0, one launch (start us, length us, event | category | flops | bytes accessed | tf_op | source)
XLA Modules:
  0.0 67.8 jit_solution(2184693233959530739)
XLA Ops:
  0.6 0.0 copy-start
  0.7 0.8 %eq.28 = s32[64]{0:T(128)S(1)} reshape(s32[8,8]{1,0:T(8,128)} %param.10) | data formatting | bytes 512 | tf_op jit(solution)/shard_map/eq | solution.py:51
  1.5 0.7 %broadcast_multiply_fusion = s32[8,8]{1,0:T(8,128)S(1)} fusion(s32[8,8]{1,0:T(8,128)} %param.10), kind=kLoop, calls=%fused_computation.50 | loop fusion | flops 64 | bytes 512 | tf_op jit(solution)/shard_map/mul | solution.py:54
  2.2 0.1 mul.82
  2.3 0.1 fusion.19
  2.3 0.1 reduce_window_sum.11
  2.4 0.2 select_reduce_fusion
  2.6 0.8 %scatter_custom_fusion = s32[128]{0:T(128)S(1)} fusion(s32[64]{0:T(128)S(1)} %fusion.20, s32[64]{0:T(128)S(1)} %iota.11, s32[]{:T(128)} %constant.16.clone.1), kind=kCustom, calls=%fused_computation.62 | custom fusion | bytes 516 | tf_op jit(solution)/shard_map/scatter | solution.py:56
  3.5 0.1 broadcast_in_dim.26
  3.6 0.0 copy-start.5
  3.6 0.9 %gather_fusion = bf16[128,1024]{1,0:T(8,128)(2,1)S(1)} fusion(bf16[8,1024]{1,0:T(8,128)(2,1)S(1)} %copy-done.1, s32[1024]{0:T(1024)S(1)} %get-tuple-element.13), kind=kCustom, calls=%fused_computation | custom fusion | bytes 524800 | tf_op jit(solution)/shard_map/gather | solution.py:87
  4.5 0.1 gather.20
  4.6 0.9 %broadcast_select_fusion = bf16[32,4,1024]{2,1,0:T(4,128)(2,1)} fusion(bf16[32,4,1024]{2,1,0:T(4,128)(2,1)S(1)} %gather.20, pred[32,4]{1,0:T(8,128)(4,1)S(1)} %broadcast_in_dim.26), kind=kLoop, calls=%fused_computation.31 | loop fusion | flops 131072 | bytes 524416 | tf_op jit(solution)/shard_map/jit(_where)/select_n | solution.py:87
  5.5 7.3 %all-to-all-start = ((bf16[32,4,1024]{2,1,0:T(4,128)(2,1)}), bf16[32,4,1024]{2,1,0:T(4,128)(2,1)S(1)}, u32[]{:S(2)}, u32[]{:S(2)}) async-start(bf16[32,4,1024]{2,1,0:T(4,128)(2,1)} %broadcast_select_fusion), calls=%async_computation | async-start | bytes 524288 | tf_op jit(solution)/shard_map/all_to_all | solution.py:103
  12.9 0.2 select_reduce_fusion.1
  13.1 0.1 convert_multiply_fusion.1
  13.2 0.1 reshape.104
  13.2 1.2 %gather_fusion.2 = f32[128]{0:T(128)S(1)} fusion(f32[64]{0:T(128)S(1)} %reshape.104, s32[1024]{0:T(1024)S(1)} %get-tuple-element.12), kind=kCustom, calls=%fused_computation.2 | custom fusion | bytes 1536 | tf_op jit(solution)/shard_map/gather | solution.py:90
  14.5 0.1 mul.93
  14.6 0.9 %gather_fusion.3 = bf16[128,1024]{1,0:T(8,128)(2,1)S(1)} fusion(bf16[8,1024]{1,0:T(8,128)(2,1)S(1)} %copy-done.2, s32[1024]{0:T(1024)S(1)} %get-tuple-element.13), kind=kCustom, calls=%fused_computation.3 | custom fusion | bytes 524800 | tf_op jit(solution)/shard_map/gather | solution.py:91
  15.5 0.2 reshape.109
  15.7 0.9 %multiply_convert_fusion = bf16[32,4,1024]{2,1,0:T(4,128)(2,1)} fusion(f32[32,4,1024]{2,1,0:T(4,128)S(1)} %reshape.109, f32[32,4]{1,0:T(8,128)S(1)} %mul.93), kind=kLoop, calls=%fused_computation.28 | loop fusion | flops 262144 | bytes 786944 | tf_op jit(solution)/shard_map/convert_element_type | solution.py:91
  16.5 6.9 %all-to-all-done = bf16[32,4,1024]{2,1,0:T(4,128)(2,1)S(1)} async-done(((bf16[32,4,1024]{2,1,0:T(4,128)(2,1)}), bf16[32,4,1024]{2,1,0:T(4,128)(2,1)S(1)}, u32[]{:S(2)}, u32[]{:S(2)}) %all-to-all-start) | async-done | bytes 262176 | tf_op jit(solution)/shard_map/all_to_all | solution.py:103
  23.4 2.6 %all-to-all-start.2 = ((bf16[32,4,1024]{2,1,0:T(4,128)(2,1)}), bf16[32,4,1024]{2,1,0:T(4,128)(2,1)S(1)}, u32[]{:S(2)}, u32[]{:S(2)}) async-start(bf16[32,4,1024]{2,1,0:T(4,128)(2,1)} %multiply_convert_fusion), calls=%async_computation.2 | async-start | bytes 524288 | tf_op jit(solution)/shard_map/all_to_all | solution.py:113
  26.0 0.1 reshape.101
  26.1 1.0 %fusion.11 = f32[128,384]{1,0:T(8,128)} fusion(bf16[128,1024]{1,0:T(8,128)(2,1)S(1)} %reshape.101, bf16[1,1024,384]{2,1,0:T(8,128)(2,1)S(1)} %copy-done.3), kind=kOutput, calls=%fused_computation.22 | convolution fusion | flops 100663296 | bytes 1245184 | tf_op jit(solution)/shard_map/dot_general | solution.py:26
  27.1 1.0 %fusion.15 = f32[128,384]{1,0:T(8,128)} fusion(bf16[128,1024]{1,0:T(8,128)(2,1)S(1)} %reshape.101, bf16[1,1024,384]{2,1,0:T(8,128)(2,1)S(1)} %copy-done.4), kind=kOutput, calls=%fused_computation.26 | convolution fusion | flops 100663296 | bytes 1245184 | tf_op jit(solution)/shard_map/dot_general | solution.py:25
  28.1 8.5 %all-to-all-done.2 = bf16[32,4,1024]{2,1,0:T(4,128)(2,1)S(1)} async-done(((bf16[32,4,1024]{2,1,0:T(4,128)(2,1)}), bf16[32,4,1024]{2,1,0:T(4,128)(2,1)S(1)}, u32[]{:S(2)}, u32[]{:S(2)}) %all-to-all-start.2) | async-done | bytes 262176 | tf_op jit(solution)/shard_map/all_to_all | solution.py:113
  36.6 0.1 reshape.105
  36.7 1.4 %multiply_convert_fusion.1 = (bf16[128,384]{1,0:T(8,128)(2,1)S(1)}, bf16[128,384]{1,0:T(8,128)(2,1)S(1)}, bf16[128,384]{1,0:T(8,128)(2,1)S(1)}) fusion(f32[128,384]{1,0:T(8,128)} %fusion.15, f32[128,384]{1,0:T(8,128)} %fusion.11, bf16[128,1024]{1,0:T(8,128)(2,1)S(1)} %reshape.105, bf16[1,384,1024]{2,1,0:T(8,128)(2,1)S(1)} %copy-done), kind=kOutput, calls=%fused_computation.32 | convolution fusion | flops 101400576 | bytes 1736704 | tf_op jit(solution)/shard_map/dot_general | solution.py:19
  38.1 0.3 convolution_convert_fusion.3
  38.4 0.8 %reshape.102 = bf16[32,4,1024]{2,1,0:T(4,128)(2,1)} reshape(bf16[128,1024]{1,0:T(8,128)(2,1)S(1)} %convolution_convert_fusion.3) | data formatting | bytes 524288 | tf_op jit(solution)/shard_map/reshape | solution.py:107
  39.2 2.6 %all-to-all-start.1 = ((bf16[32,4,1024]{2,1,0:T(4,128)(2,1)}), bf16[32,4,1024]{2,1,0:T(4,128)(2,1)S(1)}, u32[]{:S(2)}, u32[]{:S(2)}) async-start(bf16[32,4,1024]{2,1,0:T(4,128)(2,1)} %reshape.102), calls=%async_computation.1 | async-start | bytes 524288 | tf_op jit(solution)/shard_map/all_to_all | solution.py:106
  41.8 0.4 fusion.13
  42.2 0.4 fusion.6
  42.6 0.8 %reshape.106 = bf16[32,4,1024]{2,1,0:T(4,128)(2,1)} reshape(bf16[128,1024]{1,0:T(8,128)(2,1)S(1)} %fusion.6) | data formatting | bytes 524288 | tf_op jit(solution)/shard_map/reshape | solution.py:119
  43.4 1.5 %fusion.5 = f32[1,384,1024]{2,1,0:T(8,128)} fusion(bf16[128,384]{1,0:T(8,128)(2,1)S(1)} %get-tuple-element.7, bf16[128,1024]{1,0:T(8,128)(2,1)S(1)} %reshape.105), kind=kOutput, calls=%fused_computation.14 | convolution fusion | flops 101449728 | bytes 1933312 | tf_op jit(solution)/shard_map/dot_general | solution.py:13
  44.9 7.5 %all-to-all-done.1 = bf16[32,4,1024]{2,1,0:T(4,128)(2,1)S(1)} async-done(((bf16[32,4,1024]{2,1,0:T(4,128)(2,1)}), bf16[32,4,1024]{2,1,0:T(4,128)(2,1)S(1)}, u32[]{:S(2)}, u32[]{:S(2)}) %all-to-all-start.1) | async-done | bytes 262176 | tf_op jit(solution)/shard_map/all_to_all | solution.py:106
  52.4 2.6 %all-to-all-start.3 = ((bf16[32,4,1024]{2,1,0:T(4,128)(2,1)}), bf16[32,4,1024]{2,1,0:T(4,128)(2,1)S(1)}, u32[]{:S(2)}, u32[]{:S(2)}) async-start(bf16[32,4,1024]{2,1,0:T(4,128)(2,1)} %reshape.106), calls=%async_computation.3 | async-start | bytes 524288 | tf_op jit(solution)/shard_map/all_to_all | solution.py:118
  55.0 1.5 %fusion.3 = f32[1,1024,384]{2,1,0:T(8,128)} fusion(bf16[128,1024]{1,0:T(8,128)(2,1)S(1)} %reshape.101, bf16[128,384]{1,0:T(8,128)(2,1)S(1)} %get-tuple-element.5), kind=kOutput, calls=%fused_computation.12 | convolution fusion | flops 101449728 | bytes 1933312 | tf_op jit(solution)/shard_map/dot_general | solution.py:13
  56.5 1.5 %fusion.1 = f32[1,1024,384]{2,1,0:T(8,128)} fusion(bf16[128,1024]{1,0:T(8,128)(2,1)S(1)} %reshape.101, bf16[128,384]{1,0:T(8,128)(2,1)S(1)} %get-tuple-element.6), kind=kOutput, calls=%fused_computation.10 | convolution fusion | flops 101449728 | bytes 1933312 | tf_op jit(solution)/shard_map/dot_general | solution.py:13
  58.0 0.1 reshape.103
  58.1 0.7 %gather_fusion.1 = bf16[64,1024]{1,0:T(8,128)(2,1)S(1)} fusion(bf16[128,1024]{1,0:T(8,128)(2,1)S(1)} %reshape.103, s32[1024]{0:T(1024)S(1)} %pad_clamp_fusion.1), kind=kCustom, calls=%fused_computation.1 | custom fusion | bytes 262400 | tf_op jit(solution)/shard_map/gather | solution.py:125
  58.8 6.7 %all-to-all-done.3 = bf16[32,4,1024]{2,1,0:T(4,128)(2,1)S(1)} async-done(((bf16[32,4,1024]{2,1,0:T(4,128)(2,1)}), bf16[32,4,1024]{2,1,0:T(4,128)(2,1)S(1)}, u32[]{:S(2)}, u32[]{:S(2)}) %all-to-all-start.3) | async-done | bytes 262176 | tf_op jit(solution)/shard_map/all_to_all | solution.py:118
  65.5 0.1 reshape.107
  65.6 0.7 %gather_fusion.4 = bf16[64,1024]{1,0:T(8,128)(2,1)S(1)} fusion(bf16[128,1024]{1,0:T(8,128)(2,1)S(1)} %reshape.107, s32[1024]{0:T(1024)S(1)} %pad_clamp_fusion.1), kind=kCustom, calls=%fused_computation.4 | custom fusion | bytes 262400 | tf_op jit(solution)/shard_map/gather | solution.py:128
  66.3 0.7 %bitcast_reduce_fusion = bf16[8,1024]{1,0:T(8,128)(2,1)} fusion(bf16[64,1024]{1,0:T(8,128)(2,1)S(1)} %gather_fusion.4), kind=kLoop, calls=%fused_computation.37 | loop fusion | flops 57344 | bytes 147456 | tf_op jit(solution)/shard_map/reduce_sum | solution.py:129
  67.0 0.8 %fusion.17 = bf16[8,1024]{1,0:T(8,128)(2,1)} fusion(bf16[64,1024]{1,0:T(8,128)(2,1)S(1)} %gather_fusion.1, f32[8,8]{1,0:T(8,128)S(1)} %get-tuple-element.9), kind=kLoop, calls=%fused_computation.30 | loop fusion | flops 188416 | bytes 147712 | tf_op jit(solution)/shard_map/reduce_sum | solution.py:127
  (23 shorter events, 0.1 us)
Async XLA Ops:
  0.6 36.0 %copy-start = (bf16[1,384,1024]{2,1,0:T(8,128)(2,1)S(1)}, bf16[1,384,1024]{2,1,0:T(8,128)(2,1)}, u32[]{:S(2)}) copy-start(bf16[1,384,1024]{2,1,0:T(8,128)(2,1)} %param.16) | copy-start | bytes 2359300
  0.6 2.9 %copy-start.1 = (bf16[8,1024]{1,0:T(8,128)(2,1)S(1)}, bf16[8,1024]{1,0:T(8,128)(2,1)}, u32[]{:S(2)}) copy-start(bf16[8,1024]{1,0:T(8,128)(2,1)} %param.9) | copy-start | bytes 49156
  3.6 9.3 %copy-start.6 = (s32[16]{0:T(128)S(1)}, s32[16]{0:T(128)}, u32[]{:S(2)}) copy-start(s32[16]{0:T(128)} %param.13) | copy-start | bytes 196
  3.6 9.3 %copy-start.7 = (s32[8]{0:T(128)S(1)}, s32[8]{0:T(128)}, u32[]{:S(2)}) copy-start(s32[8]{0:T(128)} %param.12) | copy-start | bytes 100
  3.6 9.5 %copy-start.5 = (s32[8,8]{1,0:T(8,128)S(1)}, s32[8,8]{1,0:T(8,128)}, u32[]{:S(2)}) copy-start(s32[8,8]{1,0:T(8,128)} %param.11) | copy-start | bytes 772
  4.5 10.1 %copy-start.2 = (bf16[8,1024]{1,0:T(8,128)(2,1)S(1)}, bf16[8,1024]{1,0:T(8,128)(2,1)}, u32[]{:S(2)}) copy-start(bf16[8,1024]{1,0:T(8,128)(2,1)} %param.17) | copy-start | bytes 49156
  5.5 17.9 %all-to-all-start = ((bf16[32,4,1024]{2,1,0:T(4,128)(2,1)}), bf16[32,4,1024]{2,1,0:T(4,128)(2,1)S(1)}, u32[]{:S(2)}, u32[]{:S(2)}) async-start(bf16[32,4,1024]{2,1,0:T(4,128)(2,1)} %broadcast_select_fusion), calls=%async_computation | async-start | bytes 524288 | tf_op jit(solution)/shard_map/all_to_all | solution.py:103
  15.5 10.6 %copy-start.3 = (bf16[1,1024,384]{2,1,0:T(8,128)(2,1)S(1)}, bf16[1,1024,384]{2,1,0:T(8,128)(2,1)}, u32[]{:S(2)}) copy-start(bf16[1,1024,384]{2,1,0:T(8,128)(2,1)} %param.15) | copy-start | bytes 2359300
  15.6 11.4 %copy-start.4 = (bf16[1,1024,384]{2,1,0:T(8,128)(2,1)S(1)}, bf16[1,1024,384]{2,1,0:T(8,128)(2,1)}, u32[]{:S(2)}) copy-start(bf16[1,1024,384]{2,1,0:T(8,128)(2,1)} %param.14) | copy-start | bytes 2359300
  23.4 13.2 %all-to-all-start.2 = ((bf16[32,4,1024]{2,1,0:T(4,128)(2,1)}), bf16[32,4,1024]{2,1,0:T(4,128)(2,1)S(1)}, u32[]{:S(2)}, u32[]{:S(2)}) async-start(bf16[32,4,1024]{2,1,0:T(4,128)(2,1)} %multiply_convert_fusion), calls=%async_computation.2 | async-start | bytes 524288 | tf_op jit(solution)/shard_map/all_to_all | solution.py:113
  39.2 13.2 %all-to-all-start.1 = ((bf16[32,4,1024]{2,1,0:T(4,128)(2,1)}), bf16[32,4,1024]{2,1,0:T(4,128)(2,1)S(1)}, u32[]{:S(2)}, u32[]{:S(2)}) async-start(bf16[32,4,1024]{2,1,0:T(4,128)(2,1)} %reshape.102), calls=%async_computation.1 | async-start | bytes 524288 | tf_op jit(solution)/shard_map/all_to_all | solution.py:106
  52.4 13.2 %all-to-all-start.3 = ((bf16[32,4,1024]{2,1,0:T(4,128)(2,1)}), bf16[32,4,1024]{2,1,0:T(4,128)(2,1)S(1)}, u32[]{:S(2)}, u32[]{:S(2)}) async-start(bf16[32,4,1024]{2,1,0:T(4,128)(2,1)} %reshape.106), calls=%async_computation.3 | async-start | bytes 524288 | tf_op jit(solution)/shard_map/all_to_all | solution.py:118
where the time goes:
time: 68.3 us; the launch traced here: 67.8 us
  waiting for transfers between devices  29.6 us (43%)
  starting transfers between devices  15.1 us (22%)
  matrix products  9.02 us (13%)
  local copies, waits for them, and re-layouts  8.53 us (12%)
  other arithmetic  4.56 us (7%)
  between operations  0.94 us (1%)
    all_to_all x1, waiting for transfers between devices, per_device(): lax.all_to_all(send_grads, 'ep', split_axis=0, concat_axis=0, tiled=True)  8.54 us
    all_to_all x1, waiting for transfers between devices, per_device(): lax.all_to_all(expert_out.reshape(experts, slot_cap, model_width), 'ep',...  7.48 us
    all_to_all x1, starting transfers between devices, per_device(): lax.all_to_all(send_rows, 'ep', split_axis=0, concat_axis=0, tiled=True)  7.33 us
    all_to_all x1, waiting for transfers between devices, per_device(): lax.all_to_all(send_rows, 'ep', split_axis=0, concat_axis=0, tiled=True)  6.89 us
    all_to_all x1, waiting for transfers between devices, per_device(): lax.all_to_all(slot_grad.reshape(experts, slot_cap, model_width), 'ep', s...  6.73 us
    dot_general x3, matrix products, contract_rows(): lax.dot_general(left_rows, right_rows, (((0,), (0,)), ((), ())), preferre...  4.6 us
    all_to_all x1, starting transfers between devices, per_device(): lax.all_to_all(send_grads, 'ep', split_axis=0, concat_axis=0, tiled=True)  2.59 us
    all_to_all x1, starting transfers between devices, per_device(): lax.all_to_all(expert_out.reshape(experts, slot_cap, model_width), 'ep',...  2.59 us
  transfers between devices with their start and end apart: 4, of which 4 were waited for; matrix products, arithmetic and copies ran while one was open for 18% of the time, Pallas kernels for 0%

commit v1 on v0

v1 whole, which is shorter than its diff:
```python
import functools
import jax
import jax.numpy as jnp
from jax import lax
from jax.experimental import pallas as pl
from jax.experimental.pallas import tpu as pltpu
from jax.sharding import PartitionSpec as P

BF = jnp.bfloat16
F32 = jnp.float32
MESH = pl.DeviceIdType.MESH


def dot(a, b, ca, cb):
    return lax.dot_general(a, b, (((ca,), (cb,)), ((), ())), preferred_element_type=F32)


def kernel(
    n_ep, lanes, n_sem,
    bid_ref, bcnt_ref, tok_ref, ids_ref, quant_ref, cot_ref, wg_hbm, wu_hbm, wd_hbm,
    lo_ref, tg_ref, gg_ref, gu_ref, gd_ref,
    gat, meta_f, wg, wu, wd, og, pa, pb, r1a, r1b, s1a, s1b, r2a, r2b, s2a, s2b, r3a, r3b, s3a, s3b, r4a, r4b,
    send_sems, recv_sems, w_sems,
):
    rows, width = tok_ref.shape
    top = ids_ref.shape[1]
    nz = n_ep // 8
    R = rows
    half = 4 * R
    group = 8 * R
    me = lax.axis_index("ep")
    z = me // 8
    rest = me % 8
    y, x, c = rest // 4, (rest // 2) % 2, rest % 2
    base = z * 8
    core_nbr = base + y * 4 + x * 2 + (1 - c)
    x_nbr = base + y * 4 + (1 - x) * 2 + c
    y_nbr = base + (1 - y) * 4 + x * 2 + c
    z_nbr = [None] + [lax.rem(z + k, nz) * 8 + rest for k in range(1, nz)]
    partners = [core_nbr, x_nbr, y_nbr] + z_nbr[1:]

    w_copies = [
        pltpu.make_async_copy(src.at[0], dst, w_sems.at[i])
        for i, (src, dst) in enumerate(((wg_hbm, wg), (wu_hbm, wu), (wd_hbm, wd)))
    ]
    for cp in w_copies:
        cp.start()

    barrier = pltpu.get_barrier_semaphore()
    for d in partners:
        pl.semaphore_signal(barrier, inc=1, device_id={"ep": d}, device_id_type=MESH)

    lane = lax.broadcasted_iota(jnp.int32, (rows, lanes), 1)
    row = lax.broadcasted_iota(jnp.int32, (rows, lanes), 0)
    count = jnp.zeros((rows, lanes), jnp.int32)
    for t in range(rows):
        count = jnp.where(row == t, bcnt_ref[bid_ref[t]], count)
    ids = ids_ref[...]
    quant = quant_ref[...]
    meta = jnp.where(lane == 2 * n_ep, count >> 5, jnp.where(lane == 2 * n_ep + 1, count & 31, 0))
    for k in range(top):
        ik = ids[:, k:k + 1]
        qk = quant[:, k:k + 1]
        meta = meta + jnp.where(lane == ik, qk >> 5, 0) + jnp.where(lane == ik + n_ep, qk & 31, 0)
    a_cols = slice(0, width + lanes)
    b_cols = slice(width + lanes, 2 * width + lanes)
    all_cols = slice(0, 2 * width + lanes)
    gat[0:R, 0:width] = tok_ref[...]
    gat[0:R, width:width + lanes] = meta.astype(F32).astype(BF)
    gat[0:R, b_cols] = cot_ref[...]

    def slot(k, cc, yy, xx):
        return k * group + cc * half + yy * 2 * R + xx * R

    pl.semaphore_wait(barrier, len(partners))

    pending = []
    counter = [0]

    def send(src, dst, target):
        i = counter[0]
        counter[0] += 1
        cp = pltpu.make_async_remote_copy(
            src_ref=src, dst_ref=dst, send_sem=send_sems.at[i], recv_sem=recv_sems.at[i],
            device_id={"ep": target}, device_id_type=MESH,
        )
        cp.start()
        pending.append(cp)
        return cp

    def g(s, cols):
        return gat.at[s:s + R, cols]

    zc = {}
    xc, yc, cc, dac, dbc = {}, {}, {}, {}, {}

    def spread(k):
        s = slot(k, 0, 0, 0)
        xc[k] = send(g(s, all_cols), g(slot(k, 0, 0, 1), all_cols), x_nbr)
        yc[k] = send(g(s, all_cols), g(slot(k, 0, 1, 0), all_cols), y_nbr)
        cc[k, 0, 0] = send(g(s, all_cols), g(slot(k, 1, 0, 0), all_cols), core_nbr)

    def diag(k):
        yc[k].wait_recv()
        s = slot(k, 0, 1, 0)
        dac[k] = send(g(s, a_cols), g(slot(k, 0, 1, 1), a_cols), x_nbr)
        cc[k, 1, 0] = send(g(s, all_cols), g(slot(k, 1, 1, 0), all_cols), core_nbr)
        xc[k].wait_recv()
        s = slot(k, 0, 0, 1)
        dbc[k] = send(g(s, b_cols), g(slot(k, 0, 1, 1), b_cols), y_nbr)
        cc[k, 0, 1] = send(g(s, all_cols), g(slot(k, 1, 0, 1), all_cols), core_nbr)

    for k in range(1, nz):
        zc[nz - k] = send(g(0, all_cols), g(slot(nz - k, 0, 0, 0), all_cols), z_nbr[k])
    spread(0)
    diag(0)
    for k in range(1, nz):
        zc[k].wait_recv()
        spread(k)
    for k in range(1, nz):
        diag(k)
    for k in range(nz):
        dac[k].wait_recv()
        dbc[k].wait_recv()
        s = slot(k, 0, 1, 1)
        cc[k, 1, 1] = send(g(s, all_cols), g(slot(k, 1, 1, 1), all_cols), core_nbr)
    for cp in w_copies:
        cp.wait()
    for k in range(nz):
        for yy in range(2):
            for xx in range(2):
                cc[k, yy, xx].wait_recv()

    toks = gat[:, 0:width]
    m = gat[:, width:width + lanes].astype(F32)
    ml = lax.broadcasted_iota(jnp.int32, m.shape, 1)
    share = jnp.sum(jnp.where(ml == me, m * 32.0, jnp.where(ml == me + n_ep, m, 0.0)), axis=1, keepdims=True) / 1024.0
    cnt = jnp.sum(jnp.where(ml == 2 * n_ep, m * 32.0, jnp.where(ml == 2 * n_ep + 1, m, 0.0)), axis=1, keepdims=True)
    scale = share * (64.0 / (64.0 + cnt))
    pre_gate = dot(toks, wg[...], 1, 0)
    pre_up = dot(toks, wu[...], 1, 0)
    sig = jax.nn.sigmoid(pre_gate)
    act = pre_gate * sig
    hidden = (act * pre_up).astype(BF)
    pa[...] = (share * dot(hidden, wd[...], 1, 0)).astype(BF)
    order = list(range(1, nz)) + [0]

    def send1(p, r1):
        return {
            k: send(p.at[k * group + half:(k + 1) * group, :], r1.at[k], core_nbr) for k in order
        }

    c1a = send1(pa, r1a)
    og[...] = (scale * gat[:, b_cols].astype(F32)).astype(BF)
    hg = dot(og[...], wd[...], 1, 1)
    gate_pre = (hg * pre_up * (sig * (1.0 + pre_gate * (1.0 - sig)))).astype(BF)
    up_pre = (hg * act).astype(BF)
    pb[...] = (dot(gate_pre, wg[...], 1, 1) + dot(up_pre, wu[...], 1, 1)).astype(BF)
    c1b = send1(pb, r1b)

    def part(ref, k, yy, xx):
        s = slot(k, 0, yy, xx)
        return ref[s:s + R, :].astype(F32)

    def sub(ref, k, yy, xx):
        s = yy * 2 * R + xx * R
        return ref[k, s:s + R, :].astype(F32)

    def one(k, yy, xx, p, r1):
        return part(p, k, yy, xx) + sub(r1, k, yy, xx)

    def step2(p, c1, r1, s1, r2, target, at):
        out = {}
        for k in order:
            c1[k].wait_recv()
            for i in range(2):
                yy, xx = at(1, i)
                s1[k, i * R:(i + 1) * R, :] = one(k, yy, xx, p, r1).astype(BF)
            out[k] = send(s1.at[k], r2.at[k], target)
        return out

    def step3(p, r1, c2, r2, s2, r3, target, at):
        out = {}
        for k in order:
            c2[k].wait_recv()
            yy, xx = at(0, 1)
            s2[k] = (one(k, yy, xx, p, r1) + r2[k, R:2 * R, :].astype(F32)).astype(BF)
            out[k] = send(s2.at[k], r3.at[k], target)
        return out

    def local(k, p, r1, r2, r3):
        return one(k, 0, 0, p, r1) + r2[k, 0:R, :].astype(F32) + r3[k].astype(F32)

    def step4(p, r1, r2, c3, r3, s3, r4):
        out = {}
        for k in order:
            c3[k].wait_recv()
            if k:
                s3[k] = local(k, p, r1, r2, r3).astype(BF)
                out[nz - k] = send(s3.at[k], r4.at[nz - k], z_nbr[k])
        return out

    def finish(p, r1, r2, r3, c4, r4, out_ref):
        total = local(0, p, r1, r2, r3)
        for k in range(1, nz):
            c4[k].wait_recv()
            total = total + r4[k].astype(F32)
        out_ref[...] = total.astype(BF)

    at_a = lambda far, i: (i, far)
    at_b = lambda far, i: (far, i)
    c2a = step2(pa, c1a, r1a, s1a, r2a, x_nbr, at_a)
    c2b = step2(pb, c1b, r1b, s1b, r2b, y_nbr, at_b)
    gg_ref[0] = dot(toks, gate_pre, 0, 0).astype(gg_ref.dtype)
    c3a = step3(pa, r1a, c2a, r2a, s2a, r3a, y_nbr, at_a)
    c3b = step3(pb, r1b, c2b, r2b, s2b, r3b, x_nbr, at_b)
    gu_ref[0] = dot(toks, up_pre, 0, 0).astype(gu_ref.dtype)
    c4a = step4(pa, r1a, r2a, c3a, r3a, s3a, r4a)
    c4b = step4(pb, r1b, r2b, c3b, r3b, s3b, r4b)
    gd_ref[0] = dot(hidden, og[...], 0, 0).astype(gd_ref.dtype)
    finish(pa, r1a, r2a, r3a, c4a, r4a, lo_ref)
    finish(pb, r1b, r2b, r3b, c4b, r4b, tg_ref)
    for cp in pending:
        cp.wait_send()
    assert counter[0] == n_sem


def per_device(
    tokens, expert_ids, gate_quant, bucket_ids, bucket_counts,
    gate_weight, up_weight, down_weight, cotangent,
):
    n_ep = lax.axis_size("ep")
    n_dp = lax.axis_size("dp")
    rows, width = tokens.shape
    if n_dp > 1:
        gate_weight, up_weight, down_weight = (
            lax.all_gather(w, "dp", axis=1, tiled=True)
            for w in (gate_weight, up_weight, down_weight)
        )
    ff = gate_weight.shape[2]
    nz = n_ep // 8
    lanes = -(-(2 * n_ep + 2) // 128) * 128
    total = n_ep * rows
    n_sem = (nz - 1) + 3 * nz + 4 * nz + nz + 2 * nz + 2 * nz + 2 * nz + 2 * (nz - 1)
    vm = pl.BlockSpec(memory_space=pltpu.VMEM)
    sm = pl.BlockSpec(memory_space=pltpu.SMEM)
    hb = pl.BlockSpec(memory_space=pltpu.HBM)
    V = pltpu.VMEM
    pair = lambda shape: [V(shape, BF), V(shape, BF)]
    outs = pl.pallas_call(
        functools.partial(kernel, n_ep, lanes, n_sem),
        out_shape=(
            jax.ShapeDtypeStruct((rows, width), BF),
            jax.ShapeDtypeStruct((rows, width), BF),
            jax.ShapeDtypeStruct((1, width, ff), BF),
            jax.ShapeDtypeStruct((1, width, ff), BF),
            jax.ShapeDtypeStruct((1, ff, width), BF),
        ),
        in_specs=[sm, sm, vm, vm, vm, vm, hb, hb, hb],
        out_specs=[vm] * 5,
        scratch_shapes=[
            V((total, 2 * width + lanes), BF),
            V((8, 128), F32),
            V((width, ff), BF),
            V((width, ff), BF),
            V((ff, width), BF),
            V((total, width), BF),
            *pair((total, width)),
            *pair((nz, 4 * rows, width)),
            *pair((nz, 2 * rows, width)),
            *pair((nz, 2 * rows, width)),
            *pair((nz, rows, width)),
            *pair((nz, rows, width)),
            *pair((nz, rows, width)),
            *pair((nz, rows, width)),
            pltpu.SemaphoreType.DMA((n_sem,)),
            pltpu.SemaphoreType.DMA((n_sem,)),
            pltpu.SemaphoreType.DMA((3,)),
        ],
        compiler_params=pltpu.CompilerParams(collective_id=0, has_side_effects=True, vmem_limit_bytes=60 * 1024 * 1024),
    )(bucket_ids, bucket_counts, tokens, expert_ids, gate_quant, cotangent, gate_weight, up_weight, down_weight)
    layer_out, token_grad, gg, gu, gd = outs
    if n_dp > 1:
        gg, gu, gd = (
            lax.psum_scatter(v, "dp", scatter_dimension=1, tiled=True) for v in (gg, gu, gd)
        )
    return (layer_out, token_grad, gg.astype(F32), gu.astype(F32), gd.astype(F32))


def solution(mesh):
    placed = (
        P(("dp", "ep"), None), P(("dp", "ep"), None), P(("dp", "ep"), None), P(("dp", "ep")), P(),
        P("ep", "dp", None), P("ep", "dp", None), P("ep", "dp", None), P(("dp", "ep"), None),
    )
    return jax.shard_map(
        per_device, mesh=mesh, in_specs=placed,
        out_specs=(
            P(("dp", "ep"), None), P(("dp", "ep"), None),
            P("ep", "dp", None), P("ep", "dp", None), P("ep", "dp", None),
        ),
        check_vma=False,
    )
```

time: 68.3 us -> 42.8 us (0.63)
  Pallas kernels: 0 us -> 35.4 us
  waiting for transfers between devices: 29.6 us -> 0 us
  starting transfers between devices: 15.1 us -> 0 us
  matrix products: 9.02 us -> 0 us
  local copies, waits for them, and re-layouts: 8.53 us -> 1.39 us
    pallas_call x0 -> x1, Pallas kernels: none -> 35.4 us  [per_device(): pl.pallas_call(functools.partial(kernel, n_ep, lanes, n_sem), out_shape=(...]
    all_to_all x4 -> x0, waiting for transfers between devices: 29.6 us -> none  [the longest x1 8.54 us: per_device(): lax.all_to_all(send_grads, 'ep', split_axis=0, concat_axis=0, tiled=True)]
    all_to_all x4 -> x0, starting transfers between devices: 15.1 us -> none  [the longest x1 7.33 us: per_device(): lax.all_to_all(send_rows, 'ep', split_axis=0, concat_axis=0, tiled=True)]
    dot_general x9 -> x0, matrix products: 9.02 us -> none  [the longest x3 4.6 us: contract_rows(): lax.dot_general(left_rows, right_rows, (((0,), (0,)), ((), ())), preferre...]
    gather x6 -> x0, local copies, waits for them, and re-layouts: 4.48 us -> none  [the longest x1 1.23 us: per_device(): scaled_flat[safe_index]]
    convert_element_type x3, other arithmetic: 0.94 us -> 5.01 us  [the longest x1 2.45 us: per_device(): gg.astype(F32)]
    reshape x7 -> x0, local copies, waits for them, and re-layouts: 1.93 us -> none  [the longest x1 0.8 us: per_device(): expert_out.reshape(experts, slot_cap, model_width)]
    reduce_sum x4 -> x0, other arithmetic: 1.81 us -> none  [the longest x1 0.76 us: per_device(): jnp.sum(gate_share[:, :, None] * out_pairs, axis=1).astype(jnp.bfloat16)]
  transfers between devices with their start and end apart: 4 -> 0, of which waited for: 4 -> 0; matrix products, arithmetic and copies ran while one was open for 18% -> 0% of each run, Pallas kernels for 0% -> 0%
where the time goes in v1:
time: 42.8 us; the launch traced here: 42.5 us
  Pallas kernels  35.4 us (83%)
  other arithmetic  5.01 us (12%)
  local copies, waits for them, and re-layouts  1.39 us (3%)
  between operations  0.66 us (2%)
    pallas_call x1, Pallas kernels, per_device(): pl.pallas_call(functools.partial(kernel, n_ep, lanes, n_sem), out_shape=(...  35.4 us
    convert_element_type x1, other arithmetic, per_device(): gg.astype(F32)  2.45 us
    unnamed x10, local copies, waits for them, and re-layouts  1.39 us
    convert_element_type x1, other arithmetic, per_device(): gd.astype(F32)  1.32 us
    convert_element_type x1, other arithmetic, per_device(): gu.astype(F32)  1.25 us

profile of v1, /device:TPU:0, one launch (start us, length us, event | category | flops | bytes accessed | tf_op | source)
XLA Modules:
  0.0 42.5 jit_solution(7715350450978502343)
XLA Ops:
  0.6 35.4 %shard_map.128 = (bf16[8,1024]{1,0:T(8,128)(2,1)}, bf16[8,1024]{1,0:T(8,128)(2,1)}, bf16[1,1024,384]{2,1,0:T(8,128)(2,1)}, bf16[1,1024,384]{2,1,0:T(8,128)(2,1)}, bf16[1,384,1024]{2,1,0:T(8,128)(2,1)}) custom-call(s32[8]{0:T(128)} %bid_ref.1, s32[16]{0:T(128)} %bcnt_ref.1, bf16[8,1024]{1,0:T(8,128)(2,1)} %tok_ref.1, s32[8,8]{1,0:T(8,128)} %ids_ref.1, ...), custom_call_target="tpu_custom_call" | custom-call | tf_op jit(solution)/shard_map/pallas_call | solution.py:250
  36.1 0.0 copy-start.1
  36.1 2.5 %convert_element_type.9 = f32[1,1024,384]{2,1,0:T(8,128)} convert(bf16[1,1024,384]{2,1,0:T(8,128)(2,1)} %get-tuple-element.12) | non-fusion elementwise | flops 393216 | bytes 2359296 | tf_op jit(solution)/shard_map/convert_element_type | solution.py:287
  38.5 0.0 copy-done.1
  38.5 0.0 copy-start
  38.5 1.2 %convert_element_type.10 = f32[1,1024,384]{2,1,0:T(8,128)} convert(bf16[1,1024,384]{2,1,0:T(8,128)(2,1)S(1)} %copy-done.1) | non-fusion elementwise | flops 393216 | bytes 2359296 | tf_op jit(solution)/shard_map/convert_element_type | solution.py:287
  39.8 0.2 copy-done
  40.0 0.0 copy-start.3
  40.0 0.0 copy-start.2
  40.0 1.3 %convert_element_type.11 = f32[1,384,1024]{2,1,0:T(8,128)} convert(bf16[1,384,1024]{2,1,0:T(8,128)(2,1)S(1)} %copy-done) | non-fusion elementwise | flops 393216 | bytes 2359296 | tf_op jit(solution)/shard_map/convert_element_type | solution.py:287
  41.3 0.0 copy-done.3
  41.3 0.6 %copy.16 = bf16[8,1024]{1,0:T(8,128)(2,1)} copy(bf16[8,1024]{1,0:T(8,128)(2,1)S(1)} %copy-done.3) | data formatting | bytes 32768
  41.9 0.0 copy-done.2
  41.9 0.6 %copy.17 = bf16[8,1024]{1,0:T(8,128)(2,1)} copy(bf16[8,1024]{1,0:T(8,128)(2,1)S(1)} %copy-done.2) | data formatting | bytes 32768
Async XLA Ops:
  36.1 2.5 %copy-start.1 = (bf16[1,1024,384]{2,1,0:T(8,128)(2,1)S(1)}, bf16[1,1024,384]{2,1,0:T(8,128)(2,1)}, u32[]{:S(2)}) copy-start(bf16[1,1024,384]{2,1,0:T(8,128)(2,1)} %get-tuple-element.13) | copy-start | bytes 2359300
  38.5 1.4 %copy-start = (bf16[1,384,1024]{2,1,0:T(8,128)(2,1)S(1)}, bf16[1,384,1024]{2,1,0:T(8,128)(2,1)}, u32[]{:S(2)}) copy-start(bf16[1,384,1024]{2,1,0:T(8,128)(2,1)} %get-tuple-element.14) | copy-start | bytes 2359300
  40.0 1.3 %copy-start.3 = (bf16[8,1024]{1,0:T(8,128)(2,1)S(1)}, bf16[8,1024]{1,0:T(8,128)(2,1)}, u32[]{:S(2)}) copy-start(bf16[8,1024]{1,0:T(8,128)(2,1)} %get-tuple-element.20) | copy-start | bytes 49156
  40.0 1.9 %copy-start.2 = (bf16[8,1024]{1,0:T(8,128)(2,1)S(1)}, bf16[8,1024]{1,0:T(8,128)(2,1)}, u32[]{:S(2)}) copy-start(bf16[8,1024]{1,0:T(8,128)(2,1)} %get-tuple-element.21) | copy-start | bytes 49156

commit v2 on v1

v2 whole, which is shorter than its diff:
```python
import functools
import jax
import jax.numpy as jnp
from jax import lax
from jax.experimental import pallas as pl
from jax.experimental.pallas import tpu as pltpu
from jax.sharding import PartitionSpec as P

BF = jnp.bfloat16
F32 = jnp.float32
MESH = pl.DeviceIdType.MESH


def dot(a, b, ca, cb):
    return lax.dot_general(a, b, (((ca,), (cb,)), ((), ())), preferred_element_type=F32)


def kernel(
    n_ep, lanes, n_sem,
    bid_hbm, bcnt_hbm, tok_hbm, ids_hbm, quant_hbm, cot_hbm, wg_hbm, wu_hbm, wd_hbm,
    lo_ref, tg_ref, gg_hbm, gu_hbm, gd_hbm,
    gat, wg, wu, wd, og, pa, pb, r1a, r1b, s1a, s1b, r2a, r2b, s2a, s2b, r3a, r3b, s3a, s3b, r4a, r4b,
    ids_v, quant_v, bid_s, bcnt_s, gg, gu, gd,
    send_sems, recv_sems, w_sems, i_sems, o_sems,
):
    R, width = tok_hbm.shape
    top = ids_hbm.shape[1]
    nz = n_ep // 8
    group = 8 * R
    me = lax.axis_index("ep")
    z = me // 8
    rest = me % 8
    y, x, c = rest // 4, (rest // 2) % 2, rest % 2
    base = z * 8
    core_nbr = base + y * 4 + x * 2 + (1 - c)
    x_nbr = base + y * 4 + (1 - x) * 2 + c
    y_nbr = base + (1 - y) * 4 + x * 2 + c
    near = [jnp.where(z < nz // 2, i, nz - i) for i in range(1, nz)]
    far = near[::-1]

    def z_at(k):
        return lax.rem(z + k, nz) * 8 + rest

    a_cols = slice(0, width + lanes)
    b_cols = slice(width + lanes, 2 * width + lanes)
    cols = {"a": a_cols, "b": b_cols}

    i_copies = [
        pltpu.make_async_copy(src, dst, i_sems.at[i])
        for i, (src, dst) in enumerate((
            (bid_hbm, bid_s), (bcnt_hbm, bcnt_s), (ids_hbm, ids_v), (quant_hbm, quant_v),
            (tok_hbm, gat.at[0, 0:R, 0:width]), (cot_hbm, gat.at[0, 0:R, b_cols]),
        ))
    ]
    for cp in i_copies:
        cp.start()
    w_copies = [
        pltpu.make_async_copy(src.at[0], dst, w_sems.at[i])
        for i, (src, dst) in enumerate(((wg_hbm, wg), (wu_hbm, wu), (wd_hbm, wd)))
    ]
    for cp in w_copies:
        cp.start()
    barrier = pltpu.get_barrier_semaphore()
    for d in [z_at(k) for k in range(1, nz)] + [core_nbr, x_nbr, y_nbr]:
        pl.semaphore_signal(barrier, inc=1, device_id={"ep": d}, device_id_type=MESH)
    for cp in i_copies:
        cp.wait()

    lane = lax.broadcasted_iota(jnp.int32, (R, lanes), 1)
    row = lax.broadcasted_iota(jnp.int32, (R, lanes), 0)
    count = jnp.zeros((R, lanes), jnp.int32)
    for t in range(R):
        count = jnp.where(row == t, bcnt_s[bid_s[t]], count)
    ids = ids_v[...]
    quant = quant_v[...]
    meta = jnp.where(lane == 2 * n_ep, count >> 5, jnp.where(lane == 2 * n_ep + 1, count & 31, 0))
    for k in range(top):
        ik = ids[:, k:k + 1]
        qk = quant[:, k:k + 1]
        meta = meta + jnp.where(lane == ik, qk >> 5, 0) + jnp.where(lane == ik + n_ep, qk & 31, 0)
    gat[0, 0:R, width:width + lanes] = meta.astype(F32).astype(BF)
    pl.semaphore_wait(barrier, nz + 2)

    pending = []
    bases = {}

    def index(name, k):
        if name not in bases:
            bases[name] = len(bases) * nz
        return bases[name] + k

    def send(name, src, dst, target, k):
        i = index(name, k)
        cp = pltpu.make_async_remote_copy(
            src_ref=src, dst_ref=dst, send_sem=send_sems.at[i], recv_sem=recv_sems.at[i],
            device_id={"ep": target}, device_id_type=MESH,
        )
        cp.start()
        pending.append(cp)

    def landed(name, dst, k):
        i = index(name, k)
        pltpu.make_async_remote_copy(
            src_ref=dst, dst_ref=dst, send_sem=send_sems.at[i], recv_sem=recv_sems.at[i],
            device_id={"ep": core_nbr}, device_id_type=MESH,
        ).wait_recv()

    def blk(h, k, cc, yy, xx):
        s = cc * 4 * R + yy * 2 * R + xx * R
        return gat.at[k, s:s + R, cols[h]]

    def to_x(h, k):
        send("x" + h, blk(h, k, 0, 0, 0), blk(h, k, 0, 0, 1), x_nbr, k)

    def to_y(h, k):
        send("y" + h, blk(h, k, 0, 0, 0), blk(h, k, 0, 1, 0), y_nbr, k)

    def to_core(h, k, yy, xx):
        send("c%d%d" % (yy, xx) + h, blk(h, k, 0, yy, xx), blk(h, k, 1, yy, xx), core_nbr, k)

    def spread(h, k):
        if h == "a":
            to_y(h, k)
            to_x(h, k)
        else:
            to_x(h, k)
            to_y(h, k)
        to_core(h, k, 0, 0)

    def start_z(h):
        for k in far:
            send("z" + h, blk(h, 0, 0, 0, 0), blk(h, nz - k, 0, 0, 0), z_at(k), nz - k)

    def pass_z(h, k):
        landed("z" + h, blk(h, k, 0, 0, 0), k)
        spread(h, k)

    def pass_xy(h, k):
        if h == "a":
            landed("y" + h, blk(h, k, 0, 1, 0), k)
            send("d" + h, blk(h, k, 0, 1, 0), blk(h, k, 0, 1, 1), x_nbr, k)
            to_core(h, k, 1, 0)
            landed("x" + h, blk(h, k, 0, 0, 1), k)
            to_core(h, k, 0, 1)
        else:
            landed("x" + h, blk(h, k, 0, 0, 1), k)
            send("d" + h, blk(h, k, 0, 0, 1), blk(h, k, 0, 1, 1), y_nbr, k)
            to_core(h, k, 0, 1)
            landed("y" + h, blk(h, k, 0, 1, 0), k)
            to_core(h, k, 1, 0)

    def pass_d(h, k):
        landed("d" + h, blk(h, k, 0, 1, 1), k)
        to_core(h, k, 1, 1)

    def all_core(h):
        for k in range(nz):
            for yy in range(2):
                for xx in range(2):
                    landed("c%d%d" % (yy, xx) + h, blk(h, k, 1, yy, xx), k)

    start_z("a")
    spread("a", 0)
    start_z("b")
    spread("b", 0)
    pass_xy("a", 0)
    for k in near:
        pass_z("a", k)
    pass_xy("b", 0)
    for k in near:
        pass_z("b", k)
    for k in near:
        pass_xy("a", k)
    pass_d("a", 0)
    for k in near:
        pass_xy("b", k)
    for k in near:
        pass_d("a", k)
    for cp in w_copies:
        cp.wait()
    all_core("a")

    total = n_ep * R
    toks = gat[:, :, 0:width].reshape(total, width)
    m = gat[:, :, width:width + lanes].reshape(total, lanes).astype(F32)
    ml = lax.broadcasted_iota(jnp.int32, m.shape, 1)
    share = jnp.sum(jnp.where(ml == me, m * 32.0, jnp.where(ml == me + n_ep, m, 0.0)), axis=1, keepdims=True) / 1024.0
    cnt = jnp.sum(jnp.where(ml == 2 * n_ep, m * 32.0, jnp.where(ml == 2 * n_ep + 1, m, 0.0)), axis=1, keepdims=True)
    scale = share * (64.0 / (64.0 + cnt))
    pre_gate = dot(toks, wg[...], 1, 0)
    pre_up = dot(toks, wu[...], 1, 0)
    pass_d("b", 0)
    for k in near:
        pass_d("b", k)
    sig = jax.nn.sigmoid(pre_gate)
    act = pre_gate * sig
    hidden = (act * pre_up).astype(BF)
    pa[...] = (share * dot(hidden, wd[...], 1, 0)).astype(BF).reshape(pa.shape)
    order = far + [0]

    def send1(h, p, r1):
        for k in order:
            send("r1" + h, p.at[k, 4 * R:8 * R, :], r1.at[k], core_nbr, k)

    send1("a", pa, r1a)
    all_core("b")
    og[...] = (scale * gat[:, :, b_cols].reshape(total, width).astype(F32)).astype(BF)
    hg = dot(og[...], wd[...], 1, 1)
    gate_pre = (hg * pre_up * (sig * (1.0 + pre_gate * (1.0 - sig)))).astype(BF)
    up_pre = (hg * act).astype(BF)

    def sub(ref, k, yy, xx):
        s = yy * 2 * R + xx * R
        return ref[k, s:s + R, :].astype(F32)

    def one(k, yy, xx, p, r1):
        return sub(p, k, yy, xx) + sub(r1, k, yy, xx)

    def step2(h, p, r1, s1, r2, target, at):
        for k in order:
            landed("r1" + h, r1.at[k], k)
            for i in range(2):
                yy, xx = at(1, i)
                s1[k, i * R:(i + 1) * R, :] = one(k, yy, xx, p, r1).astype(BF)
            send("r2" + h, s1.at[k], r2.at[k], target, k)

    def step3(h, p, r1, r2, s2, r3, target, at):
        for k in order:
            landed("r2" + h, r2.at[k], k)
            yy, xx = at(0, 1)
            s2[k] = (one(k, yy, xx, p, r1) + r2[k, R:2 * R, :].astype(F32)).astype(BF)
            send("r3" + h, s2.at[k], r3.at[k], target, k)

    def local(k, p, r1, r2, r3):
        return one(k, 0, 0, p, r1) + r2[k, 0:R, :].astype(F32) + r3[k].astype(F32)

    def step4(h, p, r1, r2, r3, s3, r4):
        for k in far:
            landed("r3" + h, r3.at[k], k)
            s3[k] = local(k, p, r1, r2, r3).astype(BF)
            send("r4" + h, s3.at[k], r4.at[nz - k], z_at(k), nz - k)
        landed("r3" + h, r3.at[0], 0)

    def finish(h, p, r1, r2, r3, r4, out_ref):
        acc = local(0, p, r1, r2, r3)
        for k in near:
            landed("r4" + h, r4.at[k], k)
            acc = acc + r4[k].astype(F32)
        out_ref[...] = acc.astype(BF)

    at_a = lambda away, i: (i, away)
    at_b = lambda away, i: (away, i)
    o_copies = []

    def weight_grad(left, right, buf, out):
        buf[...] = dot(left, right, 0, 0).astype(BF)
        cp = pltpu.make_async_copy(buf, out.at[0], o_sems.at[len(o_copies)])
        cp.start()
        o_copies.append(cp)

    step2("a", pa, r1a, s1a, r2a, x_nbr, at_a)
    pb[...] = (dot(gate_pre, wg[...], 1, 1) + dot(up_pre, wu[...], 1, 1)).astype(BF).reshape(pb.shape)
    send1("b", pb, r1b)
    weight_grad(toks, gate_pre, gg, gg_hbm)
    step2("b", pb, r1b, s1b, r2b, y_nbr, at_b)
    step3("a", pa, r1a, r2a, s2a, r3a, y_nbr, at_a)
    weight_grad(toks, up_pre, gu, gu_hbm)
    step3("b", pb, r1b, r2b, s2b, r3b, x_nbr, at_b)
    step4("a", pa, r1a, r2a, r3a, s3a, r4a)
    weight_grad(hidden, og[...], gd, gd_hbm)
    step4("b", pb, r1b, r2b, r3b, s3b, r4b)
    finish("a", pa, r1a, r2a, r3a, r4a, lo_ref)
    finish("b", pb, r1b, r2b, r3b, r4b, tg_ref)
    for cp in pending:
        cp.wait_send()
    for cp in o_copies:
        cp.wait()
    assert len(bases) * nz == n_sem


def widen(parts, lo_in, tg_in, gg_in, gu_in, gd_in, lo, tg, gg, gu, gd, gb, ub, db, gf, uf, df, in_sems, out_sems):
    lo[...] = lo_in[...]
    tg[...] = tg_in[...]
    work = []
    for w, (src, mid, wide, dst) in enumerate(((gg_in, gb, gf, gg), (gu_in, ub, uf, gu), (gd_in, db, df, gd))):
        rows = mid.shape[0] // parts
        for i in range(parts):
            at = slice(i * rows, (i + 1) * rows)
            n = w * parts + i
            cp = pltpu.make_async_copy(src.at[0, at, :], mid.at[at, :], in_sems.at[n])
            cp.start()
            out = pltpu.make_async_copy(wide.at[at, :], dst.at[0, at, :], out_sems.at[n])
            work.append((cp, out, mid, wide, at))
    for cp, out, mid, wide, at in work:
        cp.wait()
        wide[at, :] = mid[at, :].astype(F32)
        out.start()
    for item in work:
        item[1].wait()


def per_device(
    tokens, expert_ids, gate_quant, bucket_ids, bucket_counts,
    gate_weight, up_weight, down_weight, cotangent,
):
    n_ep = lax.axis_size("ep")
    n_dp = lax.axis_size("dp")
    rows, width = tokens.shape
    if n_dp > 1:
        gate_weight, up_weight, down_weight = (
            lax.all_gather(w, "dp", axis=1, tiled=True)
            for w in (gate_weight, up_weight, down_weight)
        )
    ff = gate_weight.shape[2]
    nz = n_ep // 8
    lanes = -(-(2 * n_ep + 2) // 128) * 128
    n_sem = 24 * nz
    vm = pl.BlockSpec(memory_space=pltpu.VMEM)
    hb = pl.BlockSpec(memory_space=pltpu.HBM)
    V = pltpu.VMEM
    pair = lambda shape: [V(shape, BF), V(shape, BF)]
    outs = pl.pallas_call(
        functools.partial(kernel, n_ep, lanes, n_sem),
        out_shape=(
            jax.ShapeDtypeStruct((rows, width), BF),
            jax.ShapeDtypeStruct((rows, width), BF),
            jax.ShapeDtypeStruct((1, width, ff), BF),
            jax.ShapeDtypeStruct((1, width, ff), BF),
            jax.ShapeDtypeStruct((1, ff, width), BF),
        ),
        in_specs=[hb] * 9,
        out_specs=[vm, vm, hb, hb, hb],
        scratch_shapes=[
            V((nz, 8 * rows, 2 * width + lanes), BF),
            V((width, ff), BF),
            V((width, ff), BF),
            V((ff, width), BF),
            V((n_ep * rows, width), BF),
            *pair((nz, 8 * rows, width)),
            *pair((nz, 4 * rows, width)),
            *pair((nz, 2 * rows, width)),
            *pair((nz, 2 * rows, width)),
            *pair((nz, rows, width)),
            *pair((nz, rows, width)),
            *pair((nz, rows, width)),
            *pair((nz, rows, width)),
            V(expert_ids.shape, jnp.int32),
            V(gate_quant.shape, jnp.int32),
            pltpu.SMEM(bucket_ids.shape, jnp.int32),
            pltpu.SMEM(bucket_counts.shape, jnp.int32),
            V((width, ff), BF),
            V((width, ff), BF),
            V((ff, width), BF),
            pltpu.SemaphoreType.DMA((n_sem,)),
            pltpu.SemaphoreType.DMA((n_sem,)),
            pltpu.SemaphoreType.DMA((3,)),
            pltpu.SemaphoreType.DMA((6,)),
            pltpu.SemaphoreType.DMA((3,)),
        ],
        compiler_params=pltpu.CompilerParams(collective_id=0, has_side_effects=True, vmem_limit_bytes=60 * 1024 * 1024),
    )(bucket_ids, bucket_counts, tokens, expert_ids, gate_quant, cotangent, gate_weight, up_weight, down_weight)
    layer_out, token_grad, gg, gu, gd = outs
    if n_dp > 1:
        gg, gu, gd = (
            lax.psum_scatter(v, "dp", scatter_dimension=1, tiled=True) for v in (gg, gu, gd)
        )
    parts = 2
    wide = [jax.ShapeDtypeStruct(v.shape, F32) for v in (gg, gu, gd)]
    return pl.pallas_call(
        functools.partial(widen, parts),
        out_shape=(
            jax.ShapeDtypeStruct((rows, width), BF),
            jax.ShapeDtypeStruct((rows, width), BF),
            *wide,
        ),
        in_specs=[vm, vm, hb, hb, hb],
        out_specs=[vm, vm, hb, hb, hb],
        scratch_shapes=[
            *[V(v.shape[1:], BF) for v in (gg, gu, gd)],
            *[V(v.shape[1:], F32) for v in (gg, gu, gd)],
            pltpu.SemaphoreType.DMA((3 * parts,)),
            pltpu.SemaphoreType.DMA((3 * parts,)),
        ],
        compiler_params=pltpu.CompilerParams(vmem_limit_bytes=24 * 1024 * 1024),
    )(layer_out, token_grad, gg, gu, gd)


def solution(mesh):
    placed = (
        P(("dp", "ep"), None), P(("dp", "ep"), None), P(("dp", "ep"), None), P(("dp", "ep")), P(),
        P("ep", "dp", None), P("ep", "dp", None), P("ep", "dp", None), P(("dp", "ep"), None),
    )
    return jax.shard_map(
        per_device, mesh=mesh, in_specs=placed,
        out_specs=(
            P(("dp", "ep"), None), P(("dp", "ep"), None),
            P("ep", "dp", None), P("ep", "dp", None), P("ep", "dp", None),
        ),
        check_vma=False,
    )
```

time: 42.8 us -> 43 us (level)
  other arithmetic: 5.01 us -> 0 us
  local copies, waits for them, and re-layouts: 1.39 us -> 4.83 us
  Pallas kernels: 35.4 us -> 37.2 us
    convert_element_type x3 -> x0, other arithmetic: 5.01 us -> none  [the longest x1 2.45 us: per_device(): gg.astype(F32)]
    pallas_call x0 -> x1, Pallas kernels: none -> 4.06 us  [per_device(): pl.pallas_call(functools.partial(widen, parts), out_shape=(jax.ShapeDtype...]
    unnamed x10, local copies, waits for them, and re-layouts: 1.39 us -> 4.83 us
    pallas_call x1, Pallas kernels: 35.4 us -> 33.1 us  [per_device(): pl.pallas_call(functools.partial(kernel, n_ep, lanes, n_sem), out_shape=(...]
where the time goes in v2:
time: 43 us; the launch traced here: 42.7 us
  Pallas kernels  37.2 us (87%)
  local copies, waits for them, and re-layouts  4.83 us (11%)
  between operations  0.66 us (2%)
    pallas_call x1, Pallas kernels, per_device(): pl.pallas_call(functools.partial(kernel, n_ep, lanes, n_sem), out_shape=(...  33.1 us
    unnamed x10, local copies, waits for them, and re-layouts  4.83 us
    pallas_call x1, Pallas kernels, per_device(): pl.pallas_call(functools.partial(widen, parts), out_shape=(jax.ShapeDtype...  4.06 us

profile of v2, /device:TPU:0, one launch (start us, length us, event | category | flops | bytes accessed | tf_op | source)
XLA Modules:
  0.0 42.7 jit_solution(11918459500781764587)
XLA Ops:
  0.6 33.1 %shard_map.128 = (bf16[8,1024]{1,0:T(8,128)(2,1)}, bf16[8,1024]{1,0:T(8,128)(2,1)}, bf16[1,1024,384]{2,1,0:T(8,128)(2,1)}, bf16[1,1024,384]{2,1,0:T(8,128)(2,1)}, bf16[1,384,1024]{2,1,0:T(8,128)(2,1)}) custom-call(s32[8]{0:T(128)} %bid_hbm.1, s32[16]{0:T(128)} %bcnt_hbm.1, bf16[8,1024]{1,0:T(8,128)(2,1)} %tok_hbm.1, s32[8,8]{1,0:T(8,128)} %ids_hbm.1, ...), custom_call_target="tpu_custom_call" | custom-call | tf_op jit(solution)/shard_map/pallas_call | solution.py:322
  33.8 0.0 copy-start
  33.8 1.1 %copy-done = bf16[1,1024,384]{2,1,0:T(8,128)(2,1)S(1)} copy-done((bf16[1,1024,384]{2,1,0:T(8,128)(2,1)S(1)}, bf16[1,1024,384]{2,1,0:T(8,128)(2,1)}, u32[]{:S(2)}) %copy-start) | copy-done | bytes 786456
  34.9 0.0 copy-start.1
  34.9 1.1 %copy-done.1 = bf16[1,1024,384]{2,1,0:T(8,128)(2,1)S(1)} copy-done((bf16[1,1024,384]{2,1,0:T(8,128)(2,1)S(1)}, bf16[1,1024,384]{2,1,0:T(8,128)(2,1)}, u32[]{:S(2)}) %copy-start.1) | copy-done | bytes 786456
  36.0 0.0 copy-start.2
  36.0 1.1 %copy-done.2 = bf16[1,384,1024]{2,1,0:T(8,128)(2,1)S(1)} copy-done((bf16[1,384,1024]{2,1,0:T(8,128)(2,1)S(1)}, bf16[1,384,1024]{2,1,0:T(8,128)(2,1)}, u32[]{:S(2)}) %copy-start.2) | copy-done | bytes 786456
  37.2 0.0 copy-start.3
  37.2 0.7 %copy-done.3 = bf16[8,1024]{1,0:T(8,128)(2,1)S(1)} copy-done((bf16[8,1024]{1,0:T(8,128)(2,1)S(1)}, bf16[8,1024]{1,0:T(8,128)(2,1)}, u32[]{:S(2)}) %copy-start.3) | copy-done | bytes 16408
  37.9 0.0 copy-start.4
  37.9 0.7 %copy-done.4 = bf16[8,1024]{1,0:T(8,128)(2,1)S(1)} copy-done((bf16[8,1024]{1,0:T(8,128)(2,1)S(1)}, bf16[8,1024]{1,0:T(8,128)(2,1)}, u32[]{:S(2)}) %copy-start.4) | copy-done | bytes 16408
  38.6 4.1 %shard_map.129 = (bf16[8,1024]{1,0:T(8,128)(2,1)}, bf16[8,1024]{1,0:T(8,128)(2,1)}, f32[1,1024,384]{2,1,0:T(8,128)}, f32[1,1024,384]{2,1,0:T(8,128)}, f32[1,384,1024]{2,1,0:T(8,128)}) custom-call(bf16[8,1024]{1,0:T(8,128)(2,1)S(1)} %copy-done.3, bf16[8,1024]{1,0:T(8,128)(2,1)S(1)} %copy-done.4, bf16[1,1024,384]{2,1,0:T(8,128)(2,1)S(1)} %copy-done, ...), custom_call_target="tpu_custom_call" | custom-call | tf_op jit(solution)/shard_map/pallas_call | solution.py:369
Async XLA Ops:
  33.8 1.1 %copy-start = (bf16[1,1024,384]{2,1,0:T(8,128)(2,1)S(1)}, bf16[1,1024,384]{2,1,0:T(8,128)(2,1)}, u32[]{:S(2)}) copy-start(bf16[1,1024,384]{2,1,0:T(8,128)(2,1)} %get-tuple-element.12.gg_in) | copy-start | bytes 2359300
  34.9 1.1 %copy-start.1 = (bf16[1,1024,384]{2,1,0:T(8,128)(2,1)S(1)}, bf16[1,1024,384]{2,1,0:T(8,128)(2,1)}, u32[]{:S(2)}) copy-start(bf16[1,1024,384]{2,1,0:T(8,128)(2,1)} %get-tuple-element.13.gu_in) | copy-start | bytes 2359300
  36.0 1.1 %copy-start.2 = (bf16[1,384,1024]{2,1,0:T(8,128)(2,1)S(1)}, bf16[1,384,1024]{2,1,0:T(8,128)(2,1)}, u32[]{:S(2)}) copy-start(bf16[1,384,1024]{2,1,0:T(8,128)(2,1)} %get-tuple-element.14.gd_in) | copy-start | bytes 2359300
  37.2 0.7 %copy-start.3 = (bf16[8,1024]{1,0:T(8,128)(2,1)S(1)}, bf16[8,1024]{1,0:T(8,128)(2,1)}, u32[]{:S(2)}) copy-start(bf16[8,1024]{1,0:T(8,128)(2,1)} %get-tuple-element.10.lo_in) | copy-start | bytes 49156
  37.9 0.7 %copy-start.4 = (bf16[8,1024]{1,0:T(8,128)(2,1)S(1)}, bf16[8,1024]{1,0:T(8,128)(2,1)}, u32[]{:S(2)}) copy-start(bf16[8,1024]{1,0:T(8,128)(2,1)} %get-tuple-element.11.tg_in) | copy-start | bytes 49156

commit v3 on v2

--- a/solution.py
+++ b/solution.py
@@ -43,7 +43,12 @@
 
     a_cols = slice(0, width + lanes)
     b_cols = slice(width + lanes, 2 * width + lanes)
-    cols = {"a": a_cols, "b": b_cols}
+    mid = width // 2
+    end = width + lanes
+    cols = {
+        "a": a_cols, "b": b_cols, "a0": slice(0, mid), "a1": slice(mid, end),
+        "b0": slice(end, end + mid), "b1": slice(end + mid, end + width),
+    }
 
     i_copies = [
         pltpu.make_async_copy(src, dst, i_sems.at[i])
@@ -136,21 +141,16 @@
         spread(h, k)
 
     def pass_xy(h, k):
-        if h == "a":
-            landed("y" + h, blk(h, k, 0, 1, 0), k)
-            send("d" + h, blk(h, k, 0, 1, 0), blk(h, k, 0, 1, 1), x_nbr, k)
-            to_core(h, k, 1, 0)
-            landed("x" + h, blk(h, k, 0, 0, 1), k)
-            to_core(h, k, 0, 1)
-        else:
-            landed("x" + h, blk(h, k, 0, 0, 1), k)
-            send("d" + h, blk(h, k, 0, 0, 1), blk(h, k, 0, 1, 1), y_nbr, k)
-            to_core(h, k, 0, 1)
-            landed("y" + h, blk(h, k, 0, 1, 0), k)
-            to_core(h, k, 1, 0)
+        landed("y" + h, blk(h, k, 0, 1, 0), k)
+        send("d0" + h, blk(h + "0", k, 0, 1, 0), blk(h + "0", k, 0, 1, 1), x_nbr, k)
+        to_core(h, k, 1, 0)
+        landed("x" + h, blk(h, k, 0, 0, 1), k)
+        send("d1" + h, blk(h + "1", k, 0, 0, 1), blk(h + "1", k, 0, 1, 1), y_nbr, k)
+        to_core(h, k, 0, 1)
 
     def pass_d(h, k):
-        landed("d" + h, blk(h, k, 0, 1, 1), k)
+        landed("d0" + h, blk(h + "0", k, 0, 1, 1), k)
+        landed("d1" + h, blk(h + "1", k, 0, 1, 1), k)
         to_core(h, k, 1, 1)
 
     def all_core(h):
@@ -213,33 +213,45 @@
         s = yy * 2 * R + xx * R
         return ref[k, s:s + R, :].astype(F32)
 
+    left, right = slice(0, mid), slice(mid, width)
+
     def one(k, yy, xx, p, r1):
         return sub(p, k, yy, xx) + sub(r1, k, yy, xx)
 
-    def step2(h, p, r1, s1, r2, target, at):
+    def step2(h, p, r1, s1, r2):
         for k in order:
             landed("r1" + h, r1.at[k], k)
-            for i in range(2):
-                yy, xx = at(1, i)
-                s1[k, i * R:(i + 1) * R, :] = one(k, yy, xx, p, r1).astype(BF)
-            send("r2" + h, s1.at[k], r2.at[k], target, k)
-
-    def step3(h, p, r1, r2, s2, r3, target, at):
+            corner = one(k, 1, 1, p, r1).astype(BF)
+            s1[k, 0:R, left] = one(k, 0, 1, p, r1)[:, left].astype(BF)
+            s1[k, R:2 * R, left] = corner[:, left]
+            s1[k, 0:R, right] = one(k, 1, 0, p, r1)[:, right].astype(BF)
+            s1[k, R:2 * R, right] = corner[:, right]
+            send("r2x" + h, s1.at[k, :, left], r2.at[k, :, left], x_nbr, k)
+            send("r2y" + h, s1.at[k, :, right], r2.at[k, :, right], y_nbr, k)
+
+    def step3(h, p, r1, r2, s2, r3):
         for k in order:
-            landed("r2" + h, r2.at[k], k)
-            yy, xx = at(0, 1)
-            s2[k] = (one(k, yy, xx, p, r1) + r2[k, R:2 * R, :].astype(F32)).astype(BF)
-            send("r3" + h, s2.at[k], r3.at[k], target, k)
+            landed("r2x" + h, r2.at[k, :, left], k)
+            landed("r2y" + h, r2.at[k, :, right], k)
+            away = r2[k, R:2 * R, :].astype(F32)
+            s2[k, :, left] = (one(k, 1, 0, p, r1)[:, left] + away[:, left]).astype(BF)
+            s2[k, :, right] = (one(k, 0, 1, p, r1)[:, right] + away[:, right]).astype(BF)
+            send("r3y" + h, s2.at[k, :, left], r3.at[k, :, left], y_nbr, k)
+            send("r3x" + h, s2.at[k, :, right], r3.at[k, :, right], x_nbr, k)
+
+    def landed3(h, r3, k):
+        landed("r3y" + h, r3.at[k, :, left], k)
+        landed("r3x" + h, r3.at[k, :, right], k)
 
     def local(k, p, r1, r2, r3):
         return one(k, 0, 0, p, r1) + r2[k, 0:R, :].astype(F32) + r3[k].astype(F32)
 
     def step4(h, p, r1, r2, r3, s3, r4):
         for k in far:
-            landed("r3" + h, r3.at[k], k)
+            landed3(h, r3, k)
             s3[k] = local(k, p, r1, r2, r3).astype(BF)
             send("r4" + h, s3.at[k], r4.at[nz - k], z_at(k), nz - k)
-        landed("r3" + h, r3.at[0], 0)
+        landed3(h, r3, 0)
 
     def finish(h, p, r1, r2, r3, r4, out_ref):
         acc = local(0, p, r1, r2, r3)
@@ -248,24 +260,22 @@
             acc = acc + r4[k].astype(F32)
         out_ref[...] = acc.astype(BF)
 
-    at_a = lambda away, i: (i, away)
-    at_b = lambda away, i: (away, i)
     o_copies = []
 
-    def weight_grad(left, right, buf, out):
-        buf[...] = dot(left, right, 0, 0).astype(BF)
+    def weight_grad(lhs, rhs, buf, out):
+        buf[...] = dot(lhs, rhs, 0, 0).astype(BF)
         cp = pltpu.make_async_copy(buf, out.at[0], o_sems.at[len(o_copies)])
         cp.start()
         o_copies.append(cp)
 
-    step2("a", pa, r1a, s1a, r2a, x_nbr, at_a)
+    step2("a", pa, r1a, s1a, r2a)
     pb[...] = (dot(gate_pre, wg[...], 1, 1) + dot(up_pre, wu[...], 1, 1)).astype(BF).reshape(pb.shape)
     send1("b", pb, r1b)
     weight_grad(toks, gate_pre, gg, gg_hbm)
-    step2("b", pb, r1b, s1b, r2b, y_nbr, at_b)
-    step3("a", pa, r1a, r2a, s2a, r3a, y_nbr, at_a)
+    step2("b", pb, r1b, s1b, r2b)
+    step3("a", pa, r1a, r2a, s2a, r3a)
     weight_grad(toks, up_pre, gu, gu_hbm)
-    step3("b", pb, r1b, r2b, s2b, r3b, x_nbr, at_b)
+    step3("b", pb, r1b, r2b, s2b, r3b)
     step4("a", pa, r1a, r2a, r3a, s3a, r4a)
     weight_grad(hidden, og[...], gd, gd_hbm)
     step4("b", pb, r1b, r2b, r3b, s3b, r4b)
@@ -314,7 +324,7 @@
     ff = gate_weight.shape[2]
     nz = n_ep // 8
     lanes = -(-(2 * n_ep + 2) // 128) * 128
-    n_sem = 24 * nz
+    n_sem = 30 * nz
     vm = pl.BlockSpec(memory_space=pltpu.VMEM)
     hb = pl.BlockSpec(memory_space=pltpu.HBM)
     V = pltpu.VMEM
@@ -381,7 +391,7 @@
             pltpu.SemaphoreType.DMA((3 * parts,)),
             pltpu.SemaphoreType.DMA((3 * parts,)),
         ],
-        compiler_params=pltpu.CompilerParams(vmem_limit_bytes=24 * 1024 * 1024),
+        compiler_params=pltpu.CompilerParams(vmem_limit_bytes=60 * 1024 * 1024),
     )(layer_out, token_grad, gg, gu, gd)
 
 

time: 43 us -> 38 us (0.88)
  local copies, waits for them, and re-layouts: 4.83 us -> 0 us
    unnamed x10 -> x0, local copies, waits for them, and re-layouts: 4.83 us -> none
    pallas_call x1, Pallas kernels: 33.1 us -> 32.3 us  [per_device(): pl.pallas_call(functools.partial(kernel, n_ep, lanes, n_sem), out_shape=(...]
    pallas_call x1, Pallas kernels: 4.06 us -> 4.67 us  [per_device(): pl.pallas_call(functools.partial(widen, parts), out_shape=(jax.ShapeDtype...]
where the time goes in v3:
time: 38 us; the launch traced here: 37.7 us
  Pallas kernels  37 us (97%)
  between operations  0.64 us (2%)
    pallas_call x1, Pallas kernels, per_device(): pl.pallas_call(functools.partial(kernel, n_ep, lanes, n_sem), out_shape=(...  32.3 us
    pallas_call x1, Pallas kernels, per_device(): pl.pallas_call(functools.partial(widen, parts), out_shape=(jax.ShapeDtype...  4.67 us

profile of v3, /device:TPU:0, one launch (start us, length us, event | category | flops | bytes accessed | tf_op | source)
XLA Modules:
  0.0 37.7 jit_solution(17593569567976572458)
XLA Ops:
  0.6 32.3 %shard_map.128 = (bf16[8,1024]{1,0:T(8,128)(2,1)}, bf16[8,1024]{1,0:T(8,128)(2,1)}, bf16[1,1024,384]{2,1,0:T(8,128)(2,1)}, bf16[1,1024,384]{2,1,0:T(8,128)(2,1)}, bf16[1,384,1024]{2,1,0:T(8,128)(2,1)}) custom-call(s32[8]{0:T(128)} %bid_hbm.1, s32[16]{0:T(128)} %bcnt_hbm.1, bf16[8,1024]{1,0:T(8,128)(2,1)} %tok_hbm.1, s32[8,8]{1,0:T(8,128)} %ids_hbm.1, ...), custom_call_target="tpu_custom_call" | custom-call | tf_op jit(solution)/shard_map/pallas_call | solution.py:332
  33.0 4.7 %shard_map.129 = (bf16[8,1024]{1,0:T(8,128)(2,1)}, bf16[8,1024]{1,0:T(8,128)(2,1)}, f32[1,1024,384]{2,1,0:T(8,128)}, f32[1,1024,384]{2,1,0:T(8,128)}, f32[1,384,1024]{2,1,0:T(8,128)}) custom-call(bf16[8,1024]{1,0:T(8,128)(2,1)} %get-tuple-element.10.lo_in, bf16[8,1024]{1,0:T(8,128)(2,1)} %get-tuple-element.11.tg_in, ...), custom_call_target="tpu_custom_call" | custom-call | tf_op jit(solution)/shard_map/pallas_call | solution.py:379

commit v4 on v3

--- a/solution.py
+++ b/solution.py
@@ -18,9 +18,9 @@
 def kernel(
     n_ep, lanes, n_sem,
     bid_hbm, bcnt_hbm, tok_hbm, ids_hbm, quant_hbm, cot_hbm, wg_hbm, wu_hbm, wd_hbm,
-    lo_ref, tg_ref, gg_hbm, gu_hbm, gd_hbm,
+    lo_hbm, tg_hbm, gg_hbm, gu_hbm, gd_hbm,
     gat, wg, wu, wd, og, pa, pb, r1a, r1b, s1a, s1b, r2a, r2b, s2a, s2b, r3a, r3b, s3a, s3b, r4a, r4b,
-    ids_v, quant_v, bid_s, bcnt_s, gg, gu, gd,
+    ids_v, quant_v, bid_s, bcnt_s, gg, gu, gd, lo_v, tg_v,
     send_sems, recv_sems, w_sems, i_sems, o_sems,
 ):
     R, width = tok_hbm.shape
@@ -176,6 +176,9 @@
         pass_xy("b", k)
     for k in near:
         pass_d("a", k)
+    pass_d("b", 0)
+    for k in near:
+        pass_d("b", k)
     for cp in w_copies:
         cp.wait()
     all_core("a")
@@ -189,9 +192,6 @@
     scale = share * (64.0 / (64.0 + cnt))
     pre_gate = dot(toks, wg[...], 1, 0)
     pre_up = dot(toks, wu[...], 1, 0)
-    pass_d("b", 0)
-    for k in near:
-        pass_d("b", k)
     sig = jax.nn.sigmoid(pre_gate)
     act = pre_gate * sig
     hidden = (act * pre_up).astype(BF)
@@ -253,12 +253,15 @@
             send("r4" + h, s3.at[k], r4.at[nz - k], z_at(k), nz - k)
         landed3(h, r3, 0)
 
-    def finish(h, p, r1, r2, r3, r4, out_ref):
+    def finish(h, p, r1, r2, r3, r4, buf, out):
         acc = local(0, p, r1, r2, r3)
         for k in near:
             landed("r4" + h, r4.at[k], k)
             acc = acc + r4[k].astype(F32)
-        out_ref[...] = acc.astype(BF)
+        buf[...] = acc.astype(BF)
+        cp = pltpu.make_async_copy(buf, out, o_sems.at[len(o_copies)])
+        cp.start()
+        o_copies.append(cp)
 
     o_copies = []
 
@@ -279,8 +282,8 @@
     step4("a", pa, r1a, r2a, r3a, s3a, r4a)
     weight_grad(hidden, og[...], gd, gd_hbm)
     step4("b", pb, r1b, r2b, r3b, s3b, r4b)
-    finish("a", pa, r1a, r2a, r3a, r4a, lo_ref)
-    finish("b", pb, r1b, r2b, r3b, r4b, tg_ref)
+    finish("a", pa, r1a, r2a, r3a, r4a, lo_v, lo_hbm)
+    finish("b", pb, r1b, r2b, r3b, r4b, tg_v, tg_hbm)
     for cp in pending:
         cp.wait_send()
     for cp in o_copies:
@@ -288,10 +291,9 @@
     assert len(bases) * nz == n_sem
 
 
-def widen(parts, lo_in, tg_in, gg_in, gu_in, gd_in, lo, tg, gg, gu, gd, gb, ub, db, gf, uf, df, in_sems, out_sems):
-    lo[...] = lo_in[...]
-    tg[...] = tg_in[...]
+def widen(parts, lo_in, tg_in, gg_in, gu_in, gd_in, lo, tg, gg, gu, gd, lb, tb, gb, ub, db, gf, uf, df, in_sems, out_sems):
     work = []
+    small = []
     for w, (src, mid, wide, dst) in enumerate(((gg_in, gb, gf, gg), (gu_in, ub, uf, gu), (gd_in, db, df, gd))):
         rows = mid.shape[0] // parts
         for i in range(parts):
@@ -301,11 +303,18 @@
             cp.start()
             out = pltpu.make_async_copy(wide.at[at, :], dst.at[0, at, :], out_sems.at[n])
             work.append((cp, out, mid, wide, at))
+    for i, (src, mid, dst) in enumerate(((lo_in, lb, lo), (tg_in, tb, tg))):
+        cp = pltpu.make_async_copy(src, mid, in_sems.at[3 * parts + i])
+        cp.start()
+        small.append((cp, pltpu.make_async_copy(mid, dst, out_sems.at[3 * parts + i])))
     for cp, out, mid, wide, at in work:
         cp.wait()
         wide[at, :] = mid[at, :].astype(F32)
         out.start()
-    for item in work:
+    for cp, out in small:
+        cp.wait()
+        out.start()
+    for item in work + small:
         item[1].wait()
 
 
@@ -325,7 +334,6 @@
     nz = n_ep // 8
     lanes = -(-(2 * n_ep + 2) // 128) * 128
     n_sem = 30 * nz
-    vm = pl.BlockSpec(memory_space=pltpu.VMEM)
     hb = pl.BlockSpec(memory_space=pltpu.HBM)
     V = pltpu.VMEM
     pair = lambda shape: [V(shape, BF), V(shape, BF)]
@@ -339,7 +347,7 @@
             jax.ShapeDtypeStruct((1, ff, width), BF),
         ),
         in_specs=[hb] * 9,
-        out_specs=[vm, vm, hb, hb, hb],
+        out_specs=[hb] * 5,
         scratch_shapes=[
             V((nz, 8 * rows, 2 * width + lanes), BF),
             V((width, ff), BF),
@@ -361,11 +369,12 @@
             V((width, ff), BF),
             V((width, ff), BF),
             V((ff, width), BF),
+            *pair((rows, width)),
             pltpu.SemaphoreType.DMA((n_sem,)),
             pltpu.SemaphoreType.DMA((n_sem,)),
             pltpu.SemaphoreType.DMA((3,)),
             pltpu.SemaphoreType.DMA((6,)),
-            pltpu.SemaphoreType.DMA((3,)),
+            pltpu.SemaphoreType.DMA((5,)),
         ],
         compiler_params=pltpu.CompilerParams(collective_id=0, has_side_effects=True, vmem_limit_bytes=60 * 1024 * 1024),
     )(bucket_ids, bucket_counts, tokens, expert_ids, gate_quant, cotangent, gate_weight, up_weight, down_weight)
@@ -383,13 +392,14 @@
             jax.ShapeDtypeStruct((rows, width), BF),
             *wide,
         ),
-        in_specs=[vm, vm, hb, hb, hb],
-        out_specs=[vm, vm, hb, hb, hb],
+        in_specs=[hb] * 5,
+        out_specs=[hb] * 5,
         scratch_shapes=[
+            *pair((rows, width)),
             *[V(v.shape[1:], BF) for v in (gg, gu, gd)],
             *[V(v.shape[1:], F32) for v in (gg, gu, gd)],
-            pltpu.SemaphoreType.DMA((3 * parts,)),
-            pltpu.SemaphoreType.DMA((3 * parts,)),
+            pltpu.SemaphoreType.DMA((3 * parts + 2,)),
+            pltpu.SemaphoreType.DMA((3 * parts + 2,)),
         ],
         compiler_params=pltpu.CompilerParams(vmem_limit_bytes=60 * 1024 * 1024),
     )(layer_out, token_grad, gg, gu, gd)

time: 38 us -> 36.6 us (0.963)
  Pallas kernels: 37 us -> 35.8 us
    pallas_call x1, Pallas kernels: 4.67 us -> 3.37 us  [per_device(): pl.pallas_call(functools.partial(widen, parts), out_shape=(jax.ShapeDtype...]
where the time goes in v4:
time: 36.6 us; the launch traced here: 36.4 us
  Pallas kernels  35.8 us (98%)
  between operations  0.64 us (2%)
    pallas_call x1, Pallas kernels, per_device(): pl.pallas_call(functools.partial(kernel, n_ep, lanes, n_sem), out_shape=(...  32.4 us
    pallas_call x1, Pallas kernels, per_device(): pl.pallas_call(functools.partial(widen, parts), out_shape=(jax.ShapeDtype...  3.37 us

profile of v4, /device:TPU:0, one launch (start us, length us, event | category | flops | bytes accessed | tf_op | source)
XLA Modules:
  0.0 36.4 jit_solution(15917077514883465215)
XLA Ops:
  0.6 32.4 %shard_map.128 = (bf16[8,1024]{1,0:T(8,128)(2,1)}, bf16[8,1024]{1,0:T(8,128)(2,1)}, bf16[1,1024,384]{2,1,0:T(8,128)(2,1)}, bf16[1,1024,384]{2,1,0:T(8,128)(2,1)}, bf16[1,384,1024]{2,1,0:T(8,128)(2,1)}) custom-call(s32[8]{0:T(128)} %bid_hbm.1, s32[16]{0:T(128)} %bcnt_hbm.1, bf16[8,1024]{1,0:T(8,128)(2,1)} %tok_hbm.1, s32[8,8]{1,0:T(8,128)} %ids_hbm.1, ...), custom_call_target="tpu_custom_call" | custom-call | tf_op jit(solution)/shard_map/pallas_call | solution.py:340
  33.0 3.4 %shard_map.129 = (bf16[8,1024]{1,0:T(8,128)(2,1)}, bf16[8,1024]{1,0:T(8,128)(2,1)}, f32[1,1024,384]{2,1,0:T(8,128)}, f32[1,1024,384]{2,1,0:T(8,128)}, f32[1,384,1024]{2,1,0:T(8,128)}) custom-call(bf16[8,1024]{1,0:T(8,128)(2,1)} %get-tuple-element.10.lo_in, bf16[8,1024]{1,0:T(8,128)(2,1)} %get-tuple-element.11.tg_in, ...), custom_call_target="tpu_custom_call" | custom-call | tf_op jit(solution)/shard_map/pallas_call | solution.py:388
